TPU v7x, 8 devices: a whole 2x2x1 slice. The times are simulated.
8 devices in a mesh: dp: 1 (over z), tp: 2 (over y), cp: 4 (over x, core).
Axes of the slice: x: 2, y: 2, z: 1, core: 2. Of those that a mesh axis runs over, the one named last changes fastest.
Arguments:
- x_tokens: bfloat16 [512, 5120], P(('dp', 'cp', 'tp'))
- w_q: bfloat16 [5120, 40, 128], P(None, 'tp')
- w_k: bfloat16 [5120, 40, 128], P(None, 'tp')
- w_v: bfloat16 [5120, 40, 128], P(None, 'tp')
- w_o: bfloat16 [40, 128, 5120], P('tp')
Outputs:
- output: bfloat16 [512, 5120], P(('dp', 'cp', 'tp'))
All inputs are finite; a program needn't handle non-finite values.
Results may differ from a plain program's by a relative error of at most 0.00536832.
Values are sent between devices in bfloat16 or wider.
A program may use at most 1 GiB of HBM per device.

v0:
```python
import jax
import jax.numpy as jnp
from jax import lax
from jax.sharding import PartitionSpec as P

NEG_BIG = -1e30


def online_update(q_blk, k_blk, v_blk, softmax_state, causal_mask):
    row_max, row_sum, out_acc = softmax_state
    inv_sqrt = q_blk.shape[-1] ** -0.5
    scores = jnp.einsum('qhe,khe->hqk', q_blk, k_blk, preferred_element_type=jnp.float32) * inv_sqrt
    if causal_mask is not None:
        scores = jnp.where(causal_mask, scores, NEG_BIG)
    new_max = jnp.maximum(row_max, scores.max(axis=-1))
    rescale = jnp.exp(row_max - new_max)
    weights = jnp.exp(scores - new_max[..., None])
    new_sum = rescale * row_sum + weights.sum(axis=-1)
    new_acc = rescale[..., None] * out_acc + jnp.einsum('hqk,khe->hqe', weights.astype(jnp.bfloat16), v_blk, preferred_element_type=jnp.float32)
    return new_max, new_sum, new_acc


def empty_state(n_heads, n_rows, head_dim):
    return (jnp.full((n_heads, n_rows), NEG_BIG, jnp.float32), jnp.zeros((n_heads, n_rows), jnp.float32), jnp.zeros((n_heads, n_rows, head_dim), jnp.float32))


def solution(mesh):
    cp_size = mesh.shape['cp']
    send_perm = [(rank_from, (rank_from + 1) % cp_size) for rank_from in range(cp_size)]

    def device_fn(x_loc, w_q, w_k, w_v, w_o):
        x_shard = lax.all_gather(x_loc, 'tp', axis=0, tiled=True)
        shard_len = x_shard.shape[0]
        block_len = shard_len // 2
        n_heads = w_q.shape[1]
        head_dim = w_q.shape[2]

        def project(weight):
            return jnp.einsum('sd,dhe->she', x_shard, weight, preferred_element_type=jnp.float32).astype(jnp.bfloat16)

        q_all = project(w_q)
        k_all = project(w_k)
        v_all = project(w_v)
        my_rank = lax.axis_index('cp')
        row_ids = lax.broadcasted_iota(jnp.int32, (block_len, shard_len), 0)
        col_ids = lax.broadcasted_iota(jnp.int32, (block_len, shard_len), 1)
        lo_mask = col_ids[:, :block_len] <= row_ids[:, :block_len]
        hi_mask = col_ids <= row_ids + block_len
        lo_state = online_update(q_all[:block_len], k_all[:block_len], v_all[:block_len], empty_state(n_heads, block_len, head_dim), lo_mask)
        hi_state = online_update(q_all[block_len:], k_all, v_all, empty_state(n_heads, block_len, head_dim), hi_mask)
        start_state = tuple(jnp.concatenate([lo_part, hi_part], axis=1) for lo_part, hi_part in zip(lo_state, hi_state))

        def keys_before(operands):
            k_blk, v_blk, softmax_state = operands
            return online_update(q_all, k_blk[:block_len], v_blk[:block_len], softmax_state, None)

        def keys_after(operands):
            k_blk, v_blk, softmax_state = operands
            upper_state = tuple(piece[:, block_len:] for piece in softmax_state)
            updated = online_update(q_all[block_len:], k_blk, v_blk, upper_state, None)
            return tuple(jnp.concatenate([piece[:, :block_len], fresh], axis=1) for piece, fresh in zip(softmax_state, updated))

        def kv_step(step_idx, loop_carry):
            k_cur, v_cur, softmax_state = loop_carry
            k_cur, v_cur = lax.ppermute((k_cur, v_cur), 'cp', send_perm)
            rank_from = (my_rank - step_idx) % cp_size
            softmax_state = lax.cond(rank_from < my_rank, keys_before, keys_after, (k_cur, v_cur, softmax_state))
            return k_cur, v_cur, softmax_state

        final_carry = lax.fori_loop(1, cp_size, kv_step, (k_all, v_all, start_state))
        final_state = final_carry[2]
        attn_out = (final_state[2] / final_state[1][..., None]).astype(jnp.bfloat16)
        y_part = jnp.einsum('hqe,hed->qd', attn_out, w_o, preferred_element_type=jnp.float32)
        y_loc = lax.psum_scatter(y_part, 'tp', scatter_dimension=0, tiled=True)
        return y_loc.astype(jnp.bfloat16)

    seq_spec = P(('dp', 'cp', 'tp'), None)
    head_spec = P(None, 'tp', None)
    return jax.shard_map(device_fn, mesh=mesh, in_specs=(seq_spec, head_spec, head_spec, head_spec, P('tp', None, None)), out_specs=seq_spec, check_vma=False)
```

profile of v0, /device:TPU:1, one launch (start us, length us, event | category | flops | bytes accessed | tf_op | source)
XLA Modules:
  0.0 196.5 jit_solution(15272557805241792887)
XLA Ops:
  7.4 24.1 %all-gather.2.cloned.1.call-done = bf16[128,5120]{1,0:T(8,128)(2,1)} async-done(((bf16[64,5120]{1,0:T(8,128)(2,1)}), bf16[128,5120]{1,0:T(8,128)(2,1)}) %all-gather.2.cloned.1.call-update) | async-done | bytes 1310736 | tf_op jit(solution)/shard_map/all_gather | solution.py:32
  31.6 12.5 %convolution_convert_fusion = bf16[128,20,128]{2,0,1:T(8,128)(2,1)S(1)} fusion(bf16[5120,20,128]{2,0,1:T(8,128)(2,1)} %param.10, bf16[128,5120]{1,0:T(8,128)(2,1)} %all-gather.2.cloned.1.call-done), kind=kOutput, calls=%fused_computation.24 | convolution fusion | flops 3355770880 | bytes 28180480 | tf_op jit(solution)/shard_map/sd,dhe->she/dot_general | solution.py:39
  44.1 11.5 %convolution_convert_fusion.2 = bf16[128,20,128]{2,0,1:T(8,128)(2,1)} fusion(bf16[5120,20,128]{2,0,1:T(8,128)(2,1)} %param.11, bf16[128,5120]{1,0:T(8,128)(2,1)S(1)} %copy-done), kind=kOutput, calls=%fused_computation.26 | convolution fusion | flops 3355770880 | bytes 28180480 | tf_op jit(solution)/shard_map/sd,dhe->she/dot_general | solution.py:39
  55.6 1.7 fusion.33
  57.3 1.3 fusion.34
  59.3 10.5 %convolution_convert_fusion.1 = bf16[128,20,128]{2,0,1:T(8,128)(2,1)S(1)} fusion(bf16[5120,20,128]{2,0,1:T(8,128)(2,1)} %param.12, bf16[128,5120]{1,0:T(8,128)(2,1)S(1)} %copy-done), kind=kOutput, calls=%fused_computation.25 | convolution fusion | flops 3355770880 | bytes 28180480 | tf_op jit(solution)/shard_map/sd,dhe->she/dot_general | solution.py:39
  71.0 69.0 %while.23 = (s32[]{:T(128)}, bf16[128,20,128]{2,0,1:T(8,128)(2,1)}, bf16[128,20,128]{2,0,1:T(8,128)(2,1)}, f32[20,128]{1,0:T(8,128)S(1)}, f32[20,128]{1,0:T(8,12...) while((s32[]{:T(128)}, bf16[128,20,128]{2,0,1:T(8,128)(2,1)}, ...), condition=%wide.region_11.12_spmd, body=%wide.region_4.11_spmd.sunk | while | flops 85532176 | bytes 16865732 | solution.py:70
  71.0 2.0 %collective-permute-start = (bf16[128,20,128]{2,0,1:T(8,128)(2,1)}, bf16[128,20,128]{2,0,1:T(8,128)(2,1)S(1)}, u32[]{:S(2)}, u32[]{:S(2)}) collective-permute-start(bf16[128,20,128]{2,0,1:T(8,128)(2,1)} %get-tuple-element.373), channel_id=1, source_target_pairs={{0,1},{1,2},{2,3},{3,0},{4,5},{5,6},{6,7},{7,4}} | collective-permute-start | bytes 1966088 | tf_op jit(solution)/shard_map/while/body/eval_jaxpr/ppermute | solution.py:65
  73.0 7.5 %collective-permute-done = bf16[128,20,128]{2,0,1:T(8,128)(2,1)S(1)} collective-permute-done((bf16[128,20,128]{2,0,1:T(8,128)(2,1)}, bf16[128,20,128]{2,0,1:T(8,128)(2,1)S(1)}, u32[]{:S(2)}, u32[]{:S(2)}) %collective-permute-start) | collective-permute-done | bytes 655392 | tf_op jit(solution)/shard_map/while/body/eval_jaxpr/ppermute | solution.py:65
  80.5 7.0 %collective-permute-done.1 = bf16[128,20,128]{2,0,1:T(8,128)(2,1)S(1)} collective-permute-done((bf16[128,20,128]{2,0,1:T(8,128)(2,1)}, bf16[128,20,128]{2,0,1:T(8,128)(2,1)S(1)}, u32[]{:S(2)}, u32[]{:S(2)}) %collective-permute-start.1) | collective-permute-done | bytes 655392 | tf_op jit(solution)/shard_map/while/body/eval_jaxpr/ppermute | solution.py:65
  87.5 4.3 %conditional.2 = (f32[20,128]{1,0:T(8,128)}, f32[20,128]{1,0:T(8,128)S(1)}, f32[20,128,128]{2,1,0:T(8,128)S(1)}) conditional(s32[]{:T(128)} %convert_element_type.58, (f32[20,128]{1,0:T(8,128)S(1)}, bf16[128,20,128]{2,0,1:T(8,128)(2,1)S(1)}, bf16[128,20,128]{2,0,1:T(8,128)(2,1)S(1)}, f32[20,128]{1,0:T(8,128)S(1)}, f32[20,128,128]{2,1,0:T(8,128)S(1)}, ...), branch_computations={%region_5.7_spmd, %region_8.10_spmd} | conditional | flops 85532160 | bytes 8980504 | solution.py:67
  90.3 1.5 convolution_add_fusion.1
  92.5 0.8 copy.27
  94.2 2.5 %collective-permute-start = (bf16[128,20,128]{2,0,1:T(8,128)(2,1)}, bf16[128,20,128]{2,0,1:T(8,128)(2,1)S(1)}, u32[]{:S(2)}, u32[]{:S(2)}) collective-permute-start(bf16[128,20,128]{2,0,1:T(8,128)(2,1)} %get-tuple-element.373), channel_id=1, source_target_pairs={{0,1},{1,2},{2,3},{3,0},{4,5},{5,6},{6,7},{7,4}} | collective-permute-start | bytes 1966088 | tf_op jit(solution)/shard_map/while/body/eval_jaxpr/ppermute | solution.py:65
  96.7 7.5 %collective-permute-done = bf16[128,20,128]{2,0,1:T(8,128)(2,1)S(1)} collective-permute-done((bf16[128,20,128]{2,0,1:T(8,128)(2,1)}, bf16[128,20,128]{2,0,1:T(8,128)(2,1)S(1)}, u32[]{:S(2)}, u32[]{:S(2)}) %collective-permute-start) | collective-permute-done | bytes 655392 | tf_op jit(solution)/shard_map/while/body/eval_jaxpr/ppermute | solution.py:65
  104.2 7.0 %collective-permute-done.1 = bf16[128,20,128]{2,0,1:T(8,128)(2,1)S(1)} collective-permute-done((bf16[128,20,128]{2,0,1:T(8,128)(2,1)}, bf16[128,20,128]{2,0,1:T(8,128)(2,1)S(1)}, u32[]{:S(2)}, u32[]{:S(2)}) %collective-permute-start.1) | collective-permute-done | bytes 655392 | tf_op jit(solution)/shard_map/while/body/eval_jaxpr/ppermute | solution.py:65
  111.2 2.8 %conditional.2 = (f32[20,128]{1,0:T(8,128)}, f32[20,128]{1,0:T(8,128)S(1)}, f32[20,128,128]{2,1,0:T(8,128)S(1)}) conditional(s32[]{:T(128)} %convert_element_type.58, (f32[20,128]{1,0:T(8,128)S(1)}, bf16[128,20,128]{2,0,1:T(8,128)(2,1)S(1)}, bf16[128,20,128]{2,0,1:T(8,128)(2,1)S(1)}, f32[20,128]{1,0:T(8,128)S(1)}, f32[20,128,128]{2,1,0:T(8,128)S(1)}, ...), branch_computations={%region_5.7_spmd, %region_8.10_spmd} | conditional | flops 85532160 | bytes 8980504 | solution.py:67
  116.4 4.0 %collective-permute-start = (bf16[128,20,128]{2,0,1:T(8,128)(2,1)}, bf16[128,20,128]{2,0,1:T(8,128)(2,1)S(1)}, u32[]{:S(2)}, u32[]{:S(2)}) collective-permute-start(bf16[128,20,128]{2,0,1:T(8,128)(2,1)} %get-tuple-element.373), channel_id=1, source_target_pairs={{0,1},{1,2},{2,3},{3,0},{4,5},{5,6},{6,7},{7,4}} | collective-permute-start | bytes 1966088 | tf_op jit(solution)/shard_map/while/body/eval_jaxpr/ppermute | solution.py:65
  120.4 7.5 %collective-permute-done = bf16[128,20,128]{2,0,1:T(8,128)(2,1)S(1)} collective-permute-done((bf16[128,20,128]{2,0,1:T(8,128)(2,1)}, bf16[128,20,128]{2,0,1:T(8,128)(2,1)S(1)}, u32[]{:S(2)}, u32[]{:S(2)}) %collective-permute-start) | collective-permute-done | bytes 655392 | tf_op jit(solution)/shard_map/while/body/eval_jaxpr/ppermute | solution.py:65
  127.9 7.0 %collective-permute-done.1 = bf16[128,20,128]{2,0,1:T(8,128)(2,1)S(1)} collective-permute-done((bf16[128,20,128]{2,0,1:T(8,128)(2,1)}, bf16[128,20,128]{2,0,1:T(8,128)(2,1)S(1)}, u32[]{:S(2)}, u32[]{:S(2)}) %collective-permute-start.1) | collective-permute-done | bytes 655392 | tf_op jit(solution)/shard_map/while/body/eval_jaxpr/ppermute | solution.py:65
  134.9 2.8 %conditional.2 = (f32[20,128]{1,0:T(8,128)}, f32[20,128]{1,0:T(8,128)S(1)}, f32[20,128,128]{2,1,0:T(8,128)S(1)}) conditional(s32[]{:T(128)} %convert_element_type.58, (f32[20,128]{1,0:T(8,128)S(1)}, bf16[128,20,128]{2,0,1:T(8,128)(2,1)S(1)}, bf16[128,20,128]{2,0,1:T(8,128)(2,1)S(1)}, f32[20,128]{1,0:T(8,128)S(1)}, f32[20,128,128]{2,1,0:T(8,128)S(1)}, ...), branch_computations={%region_5.7_spmd, %region_8.10_spmd} | conditional | flops 85532160 | bytes 8980504 | solution.py:67
  140.0 11.9 %convolution_bitcast_fusion = f32[128,5120]{1,0:T(8,128)} fusion(bf16[20,128,5120]{2,1,0:T(8,128)(2,1)} %param.13, f32[20,128,128]{2,1,0:T(8,128)S(1)} %get-tuple-element.259, f32[20,128]{1,0:T(8,128)S(1)} %get-tuple-element.260), kind=kOutput, calls=%fused_computation.23 | convolution fusion | flops 3356098560 | bytes 30156800 | tf_op jit(solution)/shard_map/hqe,hed->qd/dot_general | solution.py:73
  152.0 35.4 %reduce-scatter.2.cloned.1.call-done = f32[64,5120]{1,0:T(8,128)} async-done(((f32[128,5120]{1,0:T(8,128)}), f32[64,5120]{1,0:T(8,128)}) %reduce-scatter.2.cloned.1.call-update) | async-done | bytes 1310736 | tf_op jit(solution)/shard_map/reduce_scatter | solution.py:74
  187.4 2.2 %convert_element_type.43 = bf16[64,5120]{1,0:T(8,128)(2,1)} convert(f32[64,5120]{1,0:T(8,128)} %reduce-scatter.2.cloned.1.call-done) | non-fusion elementwise | flops 327680 | bytes 1966080 | tf_op jit(solution)/shard_map/convert_element_type | solution.py:75
  (52 shorter events, 17.2 us)
Async XLA Ops:
  6.5 25.0 %all-gather.2.cloned.1.call-start = ((), (), s32[]{:S(2)}) async-start(), calls=%async_computation.1 | async-start | bytes 1966080 | tf_op jit(solution)/shard_map/all_gather | solution.py:32
  7.3 180.2 %reduce-scatter.2.cloned.1.call-start = ((), (), s32[]{:S(2)}) async-start(), calls=%async_computation.2 | async-start | bytes 3932160 | tf_op jit(solution)/shard_map/reduce_scatter | solution.py:74
  31.5 12.5 %copy-start = (bf16[128,5120]{1,0:T(8,128)(2,1)S(1)}, bf16[128,5120]{1,0:T(8,128)(2,1)}, u32[]{:S(2)}) copy-start(bf16[128,5120]{1,0:T(8,128)(2,1)} %all-gather.2.cloned.1.call-done) | copy-start | bytes 3932164
  69.8 1.0 copy-start.1
  71.0 9.5 %collective-permute-start = (bf16[128,20,128]{2,0,1:T(8,128)(2,1)}, bf16[128,20,128]{2,0,1:T(8,128)(2,1)S(1)}, u32[]{:S(2)}, u32[]{:S(2)}) collective-permute-start(bf16[128,20,128]{2,0,1:T(8,128)(2,1)} %get-tuple-element.373), channel_id=1, source_target_pairs={{0,1},{1,2},{2,3},{3,0},{4,5},{5,6},{6,7},{7,4}} | collective-permute-start | bytes 1966088 | tf_op jit(solution)/shard_map/while/body/eval_jaxpr/ppermute | solution.py:65
  73.0 14.5 %collective-permute-start.1 = (bf16[128,20,128]{2,0,1:T(8,128)(2,1)}, bf16[128,20,128]{2,0,1:T(8,128)(2,1)S(1)}, u32[]{:S(2)}, u32[]{:S(2)}) collective-permute-start(bf16[128,20,128]{2,0,1:T(8,128)(2,1)} %get-tuple-element.374), channel_id=1, source_target_pairs={{0,1},{1,2},{2,3},{3,0},{4,5},{5,6},{6,7},{7,4}} | collective-permute-start | bytes 1966088 | tf_op jit(solution)/shard_map/while/body/eval_jaxpr/ppermute | solution.py:65
  94.2 10.0 %collective-permute-start = (bf16[128,20,128]{2,0,1:T(8,128)(2,1)}, bf16[128,20,128]{2,0,1:T(8,128)(2,1)S(1)}, u32[]{:S(2)}, u32[]{:S(2)}) collective-permute-start(bf16[128,20,128]{2,0,1:T(8,128)(2,1)} %get-tuple-element.373), channel_id=1, source_target_pairs={{0,1},{1,2},{2,3},{3,0},{4,5},{5,6},{6,7},{7,4}} | collective-permute-start | bytes 1966088 | tf_op jit(solution)/shard_map/while/body/eval_jaxpr/ppermute | solution.py:65
  96.7 14.5 %collective-permute-start.1 = (bf16[128,20,128]{2,0,1:T(8,128)(2,1)}, bf16[128,20,128]{2,0,1:T(8,128)(2,1)S(1)}, u32[]{:S(2)}, u32[]{:S(2)}) collective-permute-start(bf16[128,20,128]{2,0,1:T(8,128)(2,1)} %get-tuple-element.374), channel_id=1, source_target_pairs={{0,1},{1,2},{2,3},{3,0},{4,5},{5,6},{6,7},{7,4}} | collective-permute-start | bytes 1966088 | tf_op jit(solution)/shard_map/while/body/eval_jaxpr/ppermute | solution.py:65
  116.4 11.5 %collective-permute-start = (bf16[128,20,128]{2,0,1:T(8,128)(2,1)}, bf16[128,20,128]{2,0,1:T(8,128)(2,1)S(1)}, u32[]{:S(2)}, u32[]{:S(2)}) collective-permute-start(bf16[128,20,128]{2,0,1:T(8,128)(2,1)} %get-tuple-element.373), channel_id=1, source_target_pairs={{0,1},{1,2},{2,3},{3,0},{4,5},{5,6},{6,7},{7,4}} | collective-permute-start | bytes 1966088 | tf_op jit(solution)/shard_map/while/body/eval_jaxpr/ppermute | solution.py:65
  120.4 14.5 %collective-permute-start.1 = (bf16[128,20,128]{2,0,1:T(8,128)(2,1)}, bf16[128,20,128]{2,0,1:T(8,128)(2,1)S(1)}, u32[]{:S(2)}, u32[]{:S(2)}) collective-permute-start(bf16[128,20,128]{2,0,1:T(8,128)(2,1)} %get-tuple-element.374), channel_id=1, source_target_pairs={{0,1},{1,2},{2,3},{3,0},{4,5},{5,6},{6,7},{7,4}} | collective-permute-start | bytes 1966088 | tf_op jit(solution)/shard_map/while/body/eval_jaxpr/ppermute | solution.py:65
Sparse Core Ops, SparseCore 0:
  8.8 22.6 all-gather.1
  152.1 35.2 reduce-scatter.1
where the time goes:
time: 199 us; the launch traced here: 196 us
  waiting for transfers between devices  104 us (52%)
  matrix products  55 us (28%)
  between operations  13.5 us (7%)
  starting transfers between devices  8.6 us (4%)
  other arithmetic  8.16 us (4%)
  local copies, waits for them, and re-layouts  7.24 us (4%)
    ppermute x6, waiting for transfers between devices, kv_step(): k_cur, v_cur = lax.ppermute((k_cur, v_cur), 'cp', send_perm)  43.5 us
    reduce_scatter x1, waiting for transfers between devices, device_fn(): y_loc = lax.psum_scatter(y_part, 'tp', scatter_dimension=0, tiled=True)  35.4 us
    dot_general x3, matrix products, project(): jnp.einsum('sd,dhe->she', x_shard, weight, preferred_element_type=jnp.flo...  34.5 us
    all_gather x1, waiting for transfers between devices, device_fn(): x_shard = lax.all_gather(x_loc, 'tp', axis=0, tiled=True)  24.1 us
    dot_general x1, matrix products, device_fn(): jnp.einsum('hqe,hed->qd', attn_out, w_o, preferred_element_type=jnp.float32)  11.9 us
    ppermute x6, starting transfers between devices, kv_step(): k_cur, v_cur = lax.ppermute((k_cur, v_cur), 'cp', send_perm)  8.56 us
    while x9, local copies, waits for them, and re-layouts  7.13 us
    dot_general x5, matrix products, online_update(): jnp.einsum('qhe,khe->hqk', q_blk, k_blk, preferred_element_type=jnp.float32)  4.83 us
  transfers between devices with their start and end apart: 8, of which 8 were waited for; matrix products, arithmetic and copies ran while one was open for 0% of the time, Pallas kernels for 0%

commit v1 on v0

v1 whole, which is shorter than its diff:
```python
import functools

import jax
import jax.numpy as jnp
from jax import lax
from jax.experimental import pallas as pl
from jax.experimental.pallas import tpu as pltpu
from jax.sharding import PartitionSpec as P

BF16, F32 = jnp.bfloat16, jnp.float32
NEG_BIG = -1e30
D = 5120
E = 128
HEADS = 5
HE = HEADS * E
NQKV = 3 * HE
BLK = 64
NK = 4
KC = D // NK
NOUT = 10
NC = D // NOUT
MESH = pl.DeviceIdType.MESH


def remote(src, dst, send_sem, recv_sem, dev):
    return pltpu.make_async_remote_copy(src_ref=src, dst_ref=dst, send_sem=send_sem, recv_sem=recv_sem, device_id=dev, device_id_type=MESH)


def kernel(x_hbm, wq_hbm, wk_hbm, wv_hbm, wo_hbm, y_hbm, xs, w, wo, qkv, acc, osend, ofull, ysend, yrecv, ykeep, yout,
           xin_sem, w_sem, wo_sem, own_send, own_recv, fwd_send, fwd_recv, dg_send, dg_recv, dgf_send, dgf_recv, o_send_sem, o_recv_sem,
           y_send_sem, y_recv_sem, out_sem):
    cp, tp = lax.axis_index('cp'), lax.axis_index('tp')
    x, c = cp // 2, cp % 2
    sib = {'cp': 2 * x + 1 - c, 'tp': tp}
    xn = {'cp': 2 * (1 - x) + c, 'tp': tp}
    xo = {'cp': 2 * (1 - x) + 1 - c, 'tp': tp}
    yn = {'cp': cp, 'tp': 1 - tp}

    def rows(group, core, first=0, n=BLK):
        return pl.ds(pl.multiple_of(group * 128 + core * BLK + first, 32), n)

    def x_in(k):
        return pltpu.make_async_copy(x_hbm.at[:, pl.ds(k * KC, KC)], xs.at[k, rows(0, c), :], xin_sem.at[k])

    for k in range(NK):
        x_in(k).start()

    def w_in(j):
        src = (wq_hbm, wk_hbm, wv_hbm)[j // HEADS].at[cp * HEADS + j % HEADS]
        return pltpu.make_async_copy(src, w.at[:, pl.ds(j * E, E)], w_sem.at[j])

    for j in range(3 * HEADS):
        w_in(j).start()

    def wo_in(n):
        return pltpu.make_async_copy(wo_hbm.at[:, pl.ds(n * NC, NC)], wo.at[n], wo_sem.at[n])

    barrier = pltpu.get_barrier_semaphore()
    for dev in (sib, xn, xo, yn):
        pl.semaphore_signal(barrier, inc=1, device_id=dev, device_id_type=MESH)
    pl.semaphore_wait(barrier, 4)

    def own(k, which):
        dev, group = ((xn, 1), (yn, 2), (sib, 0))[which]
        return remote(xs.at[k, rows(0, c), :], xs.at[k, rows(group, c), :], own_send.at[which, k], own_recv.at[which, k], dev)

    def fwd(k, which):
        return remote(xs.at[k, rows(1 + which, c), :], xs.at[k, rows(1 + which, c), :], fwd_send.at[which, k], fwd_recv.at[which, k], sib)

    def diag(k, which):
        dev = (yn, xn)[which]
        return remote(xs.at[k, rows(1 + which, c, 32 * which, 32), :], xs.at[k, rows(3, c, 32 * which, 32), :],
                      dg_send.at[which, k], dg_recv.at[which, k], dev)

    def diag_fwd(k, which):
        sl = rows(3, c, 32 * which, 32)
        return remote(xs.at[k, sl, :], xs.at[k, sl, :], dgf_send.at[which, k], dgf_recv.at[which, k], sib)

    for k in range(NK):
        x_in(k).wait()
        for which in range(3):
            own(k, which).start()

    def nat(xx, core, t):
        b = 2 * xx + core
        return jnp.where(t == 0, b, 7 - b) * BLK

    nat_of = [nat(x, 0, tp), nat(x, 1, tp), nat(1 - x, 0, tp), nat(1 - x, 1, tp),
              nat(x, 0, 1 - tp), nat(x, 1, 1 - tp), nat(1 - x, 0, 1 - tp), nat(1 - x, 1, 1 - tp)]

    def put_qkv(slot, col, n, val):
        qkv[pl.ds(pl.multiple_of(nat_of[slot], BLK), BLK), pl.ds(col, n)] = val.astype(BF16)

    NSTEPS = ((0, 512), (512, 512), (1024, 512), (1536, 384))

    for k in range(NK):
        own(k, 2).wait_recv()
    for j in range(3 * HEADS):
        w_in(j).wait()
    for n in range(NOUT):
        wo_in(n).start()

    for col, n in NSTEPS:
        val = jnp.dot(xs[0, 0:128, :], w[0:KC, col:col + n], preferred_element_type=F32)
        for k in range(1, NK):
            val += jnp.dot(xs[k, 0:128, :], w[k * KC:(k + 1) * KC, col:col + n], preferred_element_type=F32)
        put_qkv(0, col, n, val[:BLK])
        put_qkv(1, col, n, val[BLK:])

    acc[...] = jnp.zeros_like(acc)

    def accumulate(k, row, m, arow):
        kk = pl.ds(pl.multiple_of(k * KC, KC), KC)
        for col, n in NSTEPS:
            acc[arow:arow + m, col:col + n] += jnp.dot(xs[k, row:row + m, :], w[kk, col:col + n], preferred_element_type=F32)

    @pl.loop(0, NK)
    def _(k):
        for which in range(2):
            own(k, which).wait_recv()
            diag(k, which).start()
            fwd(k, which).start()
        for which in range(2):
            fwd(k, which).wait_recv()
        accumulate(k, 128, 256, 0)

    for col, n in NSTEPS:
        for s in range(4):
            put_qkv(2 + s, col, n, acc[s * BLK:(s + 1) * BLK, col:col + n])

    @pl.loop(0, NK)
    def _(k):
        for which in range(2):
            diag(k, which).wait_recv()
            diag_fwd(k, which).start()
        for which in range(2):
            diag_fwd(k, which).wait_recv()
        accumulate(k, 384, 128, 256)

    for col, n in NSTEPS:
        for s in range(2):
            put_qkv(6 + s, col, n, acc[256 + s * BLK:256 + (s + 1) * BLK, col:col + n])

    inv_sqrt = E ** -0.5

    def o_copy(b, dev_cp):
        lohi = b // 4
        return remote(osend.at[b], ofull.at[lohi, :, pl.ds(pl.multiple_of(cp * HE, E), HE)],
                      o_send_sem.at[b], o_recv_sem.at[lohi, (cp - dev_cp + 4) % 4], {'cp': dev_cp, 'tp': tp})

    def attend(i):
        length = 128 * (i + 1)
        ri = lax.broadcasted_iota(jnp.int32, (128, 128), 0)
        ci = lax.broadcasted_iota(jnp.int32, (128, 128), 1)
        mask = ci <= ri
        for h in range(HEADS):
            q = qkv[i * 128:(i + 1) * 128, h * E:(h + 1) * E]
            kk = qkv[0:length, HE + h * E:HE + (h + 1) * E]
            v = qkv[0:length, 2 * HE + h * E:2 * HE + (h + 1) * E]
            s = lax.dot_general(q, kk, (((1,), (1,)), ((), ())), preferred_element_type=F32) * inv_sqrt
            last = jnp.where(mask, s[:, length - 128:], NEG_BIG)
            s = last if i == 0 else jnp.concatenate([s[:, :length - 128], last], axis=1)
            m = jnp.max(s, axis=-1, keepdims=True)
            p = jnp.exp(s - m)
            l = jnp.sum(p, axis=-1, keepdims=True)
            o = (jnp.dot(p.astype(BF16), v, preferred_element_type=F32) / l).astype(BF16)
            osend[2 * i, :, h * E:(h + 1) * E] = o[:BLK]
            osend[2 * i + 1, :, h * E:(h + 1) * E] = o[BLK:]
        for b in (2 * i, 2 * i + 1):
            r = b if b < 4 else 7 - b

            @pl.when(cp == r)
            def _():
                ofull[b // 4, :, pl.ds(pl.multiple_of(cp * HE, E), HE)] = osend[b]

            @pl.when(cp != r)
            def _():
                o_copy(b, r).start()

    def wait_o(lohi):
        for d in range(1, 4):
            remote(osend.at[0], ofull.at[0, :, pl.ds(0, HE)], o_send_sem.at[0], o_recv_sem.at[lohi, d], sib).wait_recv()

    @pl.when(tp == 0)
    def _():
        attend(3)
        attend(2)
        attend(1)
        attend(0)

    @pl.when(tp == 1)
    def _():
        attend(1)
        attend(0)
        attend(3)
        attend(2)

    away, home = 1 - tp, tp

    def y_copy(n):
        return remote(ysend.at[n], yrecv.at[n], y_send_sem.at[n], y_recv_sem.at[n], yn)

    wait_o(away)

    @pl.loop(0, NOUT)
    def _(n):
        wo_in(n).wait()
        ysend[n] = jnp.dot(ofull[away], wo[n], preferred_element_type=F32)
        y_copy(n).start()

    wait_o(home)

    @pl.loop(0, NOUT)
    def _(n):
        ykeep[n] = jnp.dot(ofull[home], wo[n], preferred_element_type=F32)

    def out_copy(n):
        return pltpu.make_async_copy(yout.at[n], y_hbm.at[:, pl.ds(pl.multiple_of(n * NC, NC), NC)], out_sem.at[n])

    @pl.loop(0, NOUT)
    def _(n):
        y_copy(n).wait_recv()
        yout[n] = (ykeep[n] + yrecv[n]).astype(BF16)
        out_copy(n).start()

    @pl.loop(0, NK)
    def _(k):
        for which in range(3):
            own(k, which).wait_send()
        for which in range(2):
            fwd(k, which).wait_send()
            diag(k, which).wait_send()
            diag_fwd(k, which).wait_send()

    for b in range(8):
        r = b if b < 4 else 7 - b

        @pl.when(cp != r)
        def _():
            o_copy(b, r).wait_send()

    @pl.loop(0, NOUT)
    def _(n):
        y_copy(n).wait_send()
        out_copy(n).wait()


def solution(mesh):
    def device_fn(x_loc, w_q, w_k, w_v, w_o):
        dma = pltpu.SemaphoreType.DMA
        heads_major = [jnp.transpose(t, (1, 0, 2)) for t in (w_q, w_k, w_v)]
        return pl.pallas_call(
            kernel,
            name='attention_layer',
            out_shape=jax.ShapeDtypeStruct((BLK, D), BF16),
            in_specs=[pl.BlockSpec(memory_space=pl.ANY)] * 5,
            out_specs=pl.BlockSpec(memory_space=pl.ANY),
            scratch_shapes=[
                pltpu.VMEM((NK, 512, KC), BF16),
                pltpu.VMEM((D, NQKV), BF16),
                pltpu.VMEM((NOUT, 20 * E, NC), BF16),
                pltpu.VMEM((512, NQKV), BF16),
                pltpu.VMEM((384, NQKV), F32),
                pltpu.VMEM((8, BLK, HE), BF16),
                pltpu.VMEM((2, BLK, 20 * E), BF16),
                pltpu.VMEM((NOUT, BLK, NC), F32),
                pltpu.VMEM((NOUT, BLK, NC), F32),
                pltpu.VMEM((NOUT, BLK, NC), F32),
                pltpu.VMEM((NOUT, BLK, NC), BF16),
                dma((NK,)), dma((3 * HEADS,)), dma((NOUT,)),
                dma((3, NK)), dma((3, NK)),
                dma((2, NK)), dma((2, NK)),
                dma((2, NK)), dma((2, NK)),
                dma((2, NK)), dma((2, NK)),
                dma((8,)), dma((2, 4)),
                dma((NOUT,)), dma((NOUT,)), dma((NOUT,)),
            ],
            compiler_params=pltpu.CompilerParams(collective_id=0, has_side_effects=True, vmem_limit_bytes=67043328),
        )(x_loc, *heads_major, w_o.reshape(20 * E, D))

    seq_spec = P(('dp', 'cp', 'tp'), None)
    head_spec = P(None, 'tp', None)
    return jax.shard_map(device_fn, mesh=mesh, in_specs=(seq_spec, head_spec, head_spec, head_spec, P('tp', None, None)), out_specs=seq_spec, check_vma=False)
```

time: 199 us -> 75.2 us (0.38); the launches traced: 196 us -> 74.9 us
  waiting for transfers between devices: 104 us -> 0 us
  Pallas kernels: 0 us -> 73 us
  matrix products: 55 us -> 0 us
  between operations: 13.5 us -> 0.01 us
  starting transfers between devices: 8.6 us -> 0 us
  other arithmetic: 8.16 us -> 0 us
  local copies, waits for them, and re-layouts: 7.24 us -> 1.97 us
    pallas_call x0 -> x1, Pallas kernels: none -> 73 us  [device_fn(): pl.pallas_call(kernel, name='attention_layer', out_shape=jax.ShapeDtypeSt...]
    dot_general x14 -> x0, matrix products: 55 us -> none  [the longest x3 34.5 us: project(): jnp.einsum('sd,dhe->she', x_shard, weight, preferred_element_type=jnp.flo...]
    ppermute x6 -> x0, waiting for transfers between devices: 43.5 us -> none  [kv_step(): k_cur, v_cur = lax.ppermute((k_cur, v_cur), 'cp', send_perm)]
    reduce_scatter x1 -> x0, waiting for transfers between devices: 35.4 us -> none  [device_fn(): y_loc = lax.psum_scatter(y_part, 'tp', scatter_dimension=0, tiled=True)]
    all_gather x1 -> x0, waiting for transfers between devices: 24.1 us -> none  [device_fn(): x_shard = lax.all_gather(x_loc, 'tp', axis=0, tiled=True)]
    ppermute x6 -> x0, starting transfers between devices: 8.56 us -> none  [kv_step(): k_cur, v_cur = lax.ppermute((k_cur, v_cur), 'cp', send_perm)]
    while x9 -> x0, local copies, waits for them, and re-layouts: 7.13 us -> none
    reduce_sum x5 -> x0, other arithmetic: 2.34 us -> none  [online_update(): new_sum = rescale * row_sum + weights.sum(axis=-1)]
  transfers between devices with their start and end apart: 8 -> 0, of which waited for: 8 -> 0; matrix products, arithmetic and copies ran while one was open for 0% -> 0% of each run, Pallas kernels for 0% -> 0%
where the time goes in v1:
time: 75.2 us; the launch traced here: 74.9 us
  Pallas kernels  73 us (97%)
  local copies, waits for them, and re-layouts  1.97 us (3%)
    pallas_call x1, Pallas kernels, device_fn(): pl.pallas_call(kernel, name='attention_layer', out_shape=jax.ShapeDtypeSt...  73 us
    unnamed x1, local copies, waits for them, and re-layouts  1.97 us

profile of v1, /device:TPU:1, one launch (start us, length us, event | category | flops | bytes accessed | tf_op | source)
XLA Modules:
  0.0 74.9 jit_solution(12157695564138134761)
XLA Ops:
  0.0 73.0 %attention_layer.1 = bf16[64,5120]{1,0:T(8,128)(2,1)} custom-call(bf16[64,5120]{1,0:T(8,128)(2,1)} %x_hbm.1, bf16[20,5120,128]{2,1,0:T(8,128)(2,1)} %bitcast.4, bf16[20,5120,128]{2,1,0:T(8,128)(2,1)} %bitcast.5, bf16[20,5120,128]{2,1,0:T(8,128)(2,1)} %bitcast.6, bf16[2560,5120]{1,0:T(8,128)(2,1)} %bitcast.7), custom_call_target="tpu_custom_call" | custom-call | tf_op jit(solution)/shard_map/attention_layer/pallas_call | solution.py:252
  73.0 2.0 %copy.7 = bf16[64,5120]{1,0:T(8,128)(2,1)} copy(bf16[64,5120]{1,0:T(8,128)(2,1)} %attention_layer.1) | data formatting | bytes 1310720
